TPU v7x, 32 devices: a whole 2x2x4 slice. The times are simulated.
32 devices in a mesh: tp: 8 (over z, y), dp: 4 (over x, core).
Axes of the slice: x: 2, y: 2, z: 4, core: 2. Of those that a mesh axis runs over, the one named last changes fastest.
Arguments:
- x: bfloat16 [8192, 2048], P(('dp', 'tp'))
- w_gate: bfloat16 [2048, 8192], P('dp', 'tp')
- w_up: bfloat16 [2048, 8192], P('dp', 'tp')
- w_down: bfloat16 [8192, 2048], P('tp', 'dp')
- dy: bfloat16 [8192, 2048], P(('dp', 'tp'))
Outputs:
- output 1: bfloat16 [8192, 2048], P(('dp', 'tp'))
- output 2: bfloat16 [8192, 2048], P(('dp', 'tp'))
- output 3: float32 [2048, 8192], P('dp', 'tp')
- output 4: float32 [2048, 8192], P('dp', 'tp')
- output 5: float32 [8192, 2048], P('tp', 'dp')
All inputs are finite; a program needn't handle non-finite values.
Results may differ from a plain program's by a relative error of at most 0.00111.
Values are sent between devices in bfloat16 or wider.
A program may use at most 1 GiB of HBM per device.

v0:
```python
import jax
import jax.numpy as jnp
from jax import lax
from jax.sharding import PartitionSpec as P


def solution(mesh):
    nx = mesh.shape["dp"]
    ny = mesh.shape["tp"]
    rows = P(("dp", "tp"), None)
    wsp = P("dp", "tp")
    dsp = P("tp", "dp")
    f32 = jnp.float32
    bf = jnp.bfloat16

    def to_columns(v):
        tl = v.shape[0]
        dl = v.shape[1] // nx
        vr = v.reshape(tl, nx, dl).transpose(1, 0, 2)
        return lax.all_to_all(vr, "dp", 0, 0, tiled=True)

    def from_columns(v):
        tl = v.shape[1]
        dl = v.shape[2]
        vr = lax.all_to_all(v, "dp", 0, 0, tiled=True)
        return vr.transpose(1, 0, 2).reshape(tl, nx * dl)

    def all_tokens(va):
        vg = lax.all_gather(va, "tp", axis=0, tiled=False)
        tl = vg.shape[2]
        dl = vg.shape[3]
        return vg.transpose(1, 0, 2, 3).reshape(nx * ny * tl, dl)

    def combine_tp(q, res):
        dl = q.shape[1]
        tl = q.shape[0] // (nx * ny)
        qs = lax.psum_scatter(q.reshape(nx, ny, tl, dl), "tp", scatter_dimension=1, tiled=True)
        out = res.astype(f32) + qs.reshape(nx, tl, dl)
        return from_columns(out.astype(bf))

    def local(x, w_gate, w_up, w_down, dy):
        fl = w_gate.shape[1]
        w = jnp.concatenate([w_gate, w_up], axis=1)
        xa = to_columns(x)
        xt = all_tokens(xa)
        p = lax.psum_scatter(jnp.dot(xt, w, preferred_element_type=f32), "dp", scatter_dimension=0, tiled=True)
        a = p[:, :fl]
        b = p[:, fl:]
        sig = jax.nn.sigmoid(a)
        sa = a * sig
        h = (sa * b).astype(bf)
        hg = lax.all_gather(h, "dp", axis=0, tiled=True)
        y = combine_tp(jnp.dot(hg, w_down, preferred_element_type=f32), xa)
        dya = to_columns(dy)
        dyt = all_tokens(dya)
        g = lax.psum_scatter(jnp.dot(dyt, w_down.T, preferred_element_type=f32), "dp", scatter_dimension=0, tiled=True)
        da = (g * b * sig * (1.0 + a * (1.0 - sig))).astype(bf)
        db = (g * sa).astype(bf)
        dab = lax.all_gather(jnp.concatenate([da, db], axis=1), "dp", axis=0, tiled=True)
        dx = combine_tp(jnp.dot(dab, w.T, preferred_element_type=f32), dya)
        dw = jnp.dot(xt.T, dab, preferred_element_type=f32)
        dw_down = jnp.dot(hg.T, dyt, preferred_element_type=f32)
        return y, dx, dw[:, :fl], dw[:, fl:], dw_down

    return jax.shard_map(local, mesh=mesh, in_specs=(rows, wsp, wsp, dsp, rows), out_specs=(rows, rows, wsp, wsp, dsp), check_vma=False)
```

profile of v0, /device:TPU:0, one launch (start us, length us, event | category | flops | bytes accessed | tf_op | source)
XLA Modules:
  0.0 1897.8 jit_solution(7079198349271832960)
XLA Ops:
  8.8 18.5 all_to_all.20
  31.0 17.7 all_to_all.21
  50.1 102.8 %all-gather.13.cloned.1.call-done = bf16[32,256,512]{2,1,0:T(8,128)(2,1)} async-done(((bf16[4,256,512]{2,1,0:T(8,128)(2,1)}), bf16[32,256,512]{2,1,0:T(8,128)(2,1)}) %all-gather.13.cloned.1.call-update) | async-done | bytes 8388624 | tf_op jit(solution)/shard_map/all_gather | solution.py:29
  152.9 7.5 copy.50
  160.4 17.9 fusion.5
  181.6 96.3 %all-gather.11.cloned.1.call-done = bf16[32,256,512]{2,1,0:T(8,128)(2,1)} async-done(((bf16[4,256,512]{2,1,0:T(8,128)(2,1)}), bf16[32,256,512]{2,1,0:T(8,128)(2,1)}) %all-gather.11.cloned.1.call-update) | async-done | bytes 8388624 | tf_op jit(solution)/shard_map/all_gather | solution.py:29
  277.9 7.6 copy.46
  285.5 31.1 %convolution_bitcast_fusion = f32[8192,2048]{0,1:T(8,128)} fusion(bf16[512,2048]{1,0:T(8,128)(2,1)} %constant_dynamic-update-slice_fusion, bf16[8192,512]{1,0:T(8,128)(2,1)} %bitcast.50), kind=kOutput, calls=%fused_computation | convolution fusion | flops 17179869184 | bytes 77594624 | tf_op jit(solution)/shard_map/dot_general | solution.py:46
  316.8 193.8 %reduce-scatter.9.cloned.1.call-done = f32[2048,1024]{0,1:T(8,128)} async-done(((f32[8192,1024]{0,1:T(8,128)}), f32[2048,1024]{0,1:T(8,128)}) %reduce-scatter.9.cloned.1.call-update) | async-done | bytes 8388624 | tf_op jit(solution)/shard_map/reduce_scatter | solution.py:56
  510.6 448.6 %reduce-scatter.5.cloned.1.call-done = f32[2048,2048]{0,1:T(8,128)} async-done(((f32[8192,2048]{0,1:T(8,128)}), f32[2048,2048]{0,1:T(8,128)}) %reduce-scatter.5.cloned.1.call-update) | async-done | bytes 16777232 | tf_op jit(solution)/shard_map/reduce_scatter | solution.py:46
  959.2 14.3 multiply_convert_fusion.1
  973.6 8.4 pad_maximum_fusion
  982.0 98.6 %all-gather.7.cloned.1.call-done = bf16[8192,1024]{0,1:T(8,128)(2,1)} async-done(((bf16[2048,1024]{0,1:T(8,128)(2,1)}), bf16[8192,1024]{0,1:T(8,128)(2,1)}) %all-gather.7.cloned.1.call-update) | async-done | bytes 16777232 | tf_op jit(solution)/shard_map/all_gather | solution.py:52
  1080.7 15.8 fusion.4
  1096.5 17.3 copy.47
  1114.1 170.1 %all-gather.9.cloned.1.call-done = bf16[8192,2048]{0,1:T(8,128)(2,1)} async-done(((bf16[2048,2048]{0,1:T(8,128)(2,1)}), bf16[8192,2048]{0,1:T(8,128)(2,1)}) %all-gather.9.cloned.1.call-update) | async-done | bytes 33554448 | tf_op jit(solution)/shard_map/all_gather | solution.py:59
  1284.3 27.7 %fusion.6 = f32[8192,512]{1,0:T(8,128)} fusion(bf16[8192,2048]{0,1:T(8,128)(2,1)} %all-gather.9.cloned.1.call-done, bf16[512,2048]{1,0:T(8,128)(2,1)} %constant_dynamic-update-slice_fusion), kind=kOutput, calls=%fused_computation.17 | convolution fusion | flops 17179869184 | bytes 52428800 | tf_op jit(solution)/shard_map/dot_general | solution.py:60
  1311.9 17.3 copy.52
  1329.3 237.4 %reduce-scatter.7.cloned.1.call-done = f32[4,1,256,512]{2,3,0,1:T(8,128)} async-done(((f32[4,8,256,512]{2,3,0,1:T(8,128)}), f32[4,1,256,512]{2,3,0,1:T(8,128)}) %reduce-scatter.7.cloned.1.call-update) | async-done | bytes 2097168 | tf_op jit(solution)/shard_map/reduce_scatter | solution.py:37
  1569.5 3.8 all-to-all-start.1
  1573.3 15.8 fusion.7
  1589.1 259.5 %reduce-scatter.11.cloned.1.call-done = f32[4,1,256,512]{2,3,0,1:T(8,128)} async-done(((f32[4,8,256,512]{2,3,0,1:T(8,128)}), f32[4,1,256,512]{2,3,0,1:T(8,128)}) %reduce-scatter.11.cloned.1.call-update) | async-done | bytes 2097168 | tf_op jit(solution)/shard_map/reduce_scatter | solution.py:37
  1851.5 4.2 all-to-all-start.3
  1855.8 23.7 %convolution_bitcast_fusion.1 = f32[512,2048]{0,1:T(8,128)S(1)} fusion(bf16[8192,2048]{0,1:T(8,128)(2,1)} %all-gather.9.cloned.1.call-done, bf16[8192,512]{1,0:T(8,128)(2,1)} %bitcast.51), kind=kOutput, calls=%fused_computation.7 | convolution fusion | flops 17179869184 | bytes 46137344 | tf_op jit(solution)/shard_map/dot_general | solution.py:61
  (49 shorter events, 27.2 us)
Async XLA Ops:
  7.2 153.2 %copy-start = (bf16[1024,512]{1,0:T(8,128)(2,1)S(1)}, bf16[1024,512]{1,0:T(8,128)(2,1)}, u32[]{:S(2)}) copy-start(bf16[1024,512]{1,0:T(8,128)(2,1)} %param.8) | copy-start | bytes 3145732
  7.2 145.7 %all-gather.13.cloned.1.call-start = ((), (), s32[]{:S(2)}) async-start(), calls=%async_computation.15 | async-start | bytes 9437184 | tf_op jit(solution)/shard_map/all_gather | solution.py:29
  27.3 133.1 %copy-start.2 = (bf16[4,256,512]{1,2,0:T(8,128)(2,1)}, bf16[4,256,512]{1,2,0:T(8,128)(2,1)S(1)}, u32[]{:S(2)}) copy-start(bf16[4,256,512]{1,2,0:T(8,128)(2,1)S(1)} %all_to_all.20) | copy-start | bytes 3145732
  28.7 249.2 %all-gather.11.cloned.1.call-start = ((), (), s32[]{:S(2)}) async-start(), calls=%async_computation.14 | async-start | bytes 9437184 | tf_op jit(solution)/shard_map/all_gather | solution.py:29
  48.7 111.7 %copy-start.4 = (bf16[4,256,512]{1,2,0:T(8,128)(2,1)}, bf16[4,256,512]{1,2,0:T(8,128)(2,1)S(1)}, u32[]{:S(2)}) copy-start(bf16[4,256,512]{1,2,0:T(8,128)(2,1)S(1)} %all_to_all.21) | copy-start | bytes 3145732
  50.0 460.6 %reduce-scatter.9.cloned.1.call-start = ((), (), s32[]{:S(2)}) async-start(), calls=%async_computation.11 | async-start | bytes 41943040 | tf_op jit(solution)/shard_map/reduce_scatter | solution.py:56
  178.3 1.2 copy-start.7
  178.3 2.3 copy-start.8
  178.3 780.9 %reduce-scatter.5.cloned.1.call-start = ((), (), s32[]{:S(2)}) async-start(), calls=%async_computation.8 | async-start | bytes 83886080 | tf_op jit(solution)/shard_map/reduce_scatter | solution.py:46
  316.6 764.0 %all-gather.7.cloned.1.call-start = ((), (), s32[]{:S(2)}) async-start(), calls=%async_computation.9 | async-start | bytes 20971520 | tf_op jit(solution)/shard_map/all_gather | solution.py:52
  973.5 310.7 %all-gather.9.cloned.1.call-start = ((), (), s32[]{:S(2)}) async-start(), calls=%async_computation.12 | async-start | bytes 41943040 | tf_op jit(solution)/shard_map/all_gather | solution.py:59
  982.0 584.7 %reduce-scatter.7.cloned.1.call-start = ((), (), s32[]{:S(2)}) async-start(), calls=%async_computation.10 | async-start | bytes 18874368 | tf_op jit(solution)/shard_map/reduce_scatter | solution.py:37
  1113.9 734.8 %reduce-scatter.11.cloned.1.call-start = ((), (), s32[]{:S(2)}) async-start(), calls=%async_computation.13 | async-start | bytes 18874368 | tf_op jit(solution)/shard_map/reduce_scatter | solution.py:37
  1329.3 237.4 %copy-start.5 = (bf16[4,256,512]{1,2,0:T(8,128)(2,1)S(1)}, bf16[4,256,512]{1,2,0:T(8,128)(2,1)}, u32[]{:S(2)}) copy-start(bf16[4,256,512]{1,2,0:T(8,128)(2,1)} %copy-done.4) | copy-start | bytes 3145732
  1569.5 282.0 %all-to-all-start.1 = ((bf16[4,256,512]{1,2,0:T(8,128)(2,1)}), bf16[4,256,512]{1,2,0:T(8,128)(2,1)S(1)}, u32[]{:S(2)}, u32[]{:S(2)}) async-start(bf16[4,256,512]{1,2,0:T(8,128)(2,1)} %fusion.2), calls=%async_computation.3 | async-start | bytes 2097152 | tf_op jit(solution)/shard_map/all_to_all | solution.py:25
  1573.3 275.4 %copy-start.3 = (bf16[4,256,512]{1,2,0:T(8,128)(2,1)S(1)}, bf16[4,256,512]{1,2,0:T(8,128)(2,1)}, u32[]{:S(2)}) copy-start(bf16[4,256,512]{1,2,0:T(8,128)(2,1)} %copy-done.2) | copy-start | bytes 3145732
  1851.5 4.3 copy-start.6
  1851.5 36.7 %all-to-all-start.3 = ((bf16[4,256,512]{1,2,0:T(8,128)(2,1)}), bf16[4,256,512]{1,2,0:T(8,128)(2,1)}, u32[]{:S(2)}, u32[]{:S(2)}) async-start(bf16[4,256,512]{1,2,0:T(8,128)(2,1)} %fusion.1), calls=%async_computation.7 | async-start | bytes 2097152 | tf_op jit(solution)/shard_map/all_to_all | solution.py:25
  1879.5 11.0 copy-start.1
Sparse Core Ops, SparseCore 0:
  28.8 124.0 all-gather.12
  155.6 122.2 all-gather.10
  280.5 230.0 reduce-scatter.8
  513.1 446.0 reduce-scatter.4
  973.7 106.9 all-gather.6
  1082.1 202.1 all-gather.8
  1288.0 278.6 reduce-scatter.6
  1570.5 278.1 reduce-scatter.10
where the time goes:
time: 1910 us; the launch traced here: 1900 us
  waiting for transfers between devices  1610 us (84%)
  matrix products  132 us (7%)
  local copies, waits for them, and re-layouts  70.4 us (4%)
  blocking collectives  36.2 us (2%)
  other arithmetic  28.3 us (1%)
    reduce_scatter x2, waiting for transfers between devices, combine_tp(): lax.psum_scatter(q.reshape(nx, ny, tl, dl), 'tp', scatter_dimension=1, ti...  497 us
    reduce_scatter x1, waiting for transfers between devices, local(): lax.psum_scatter(jnp.dot(xt, w, preferred_element_type=f32), 'dp', scatte...  449 us
    all_gather x2, waiting for transfers between devices, all_tokens(): vg = lax.all_gather(va, 'tp', axis=0, tiled=False)  199 us
    reduce_scatter x1, waiting for transfers between devices, local(): lax.psum_scatter(jnp.dot(dyt, w_down.T, preferred_element_type=f32), 'dp'...  194 us
    all_gather x1, waiting for transfers between devices, local(): lax.all_gather(jnp.concatenate([da, db], axis=1), 'dp', axis=0, tiled=True)  170 us
    all_gather x1, waiting for transfers between devices, local(): hg = lax.all_gather(h, 'dp', axis=0, tiled=True)  98.6 us
  transfers between devices with their start and end apart: 10, of which 8 were waited for; matrix products, arithmetic and copies ran while one was open for 11% of the time, Pallas kernels for 0%

commit v1 on v0

v1 whole, which is shorter than its diff:
```python
import jax
import jax.numpy as jnp
from jax import lax
from jax.experimental import pallas as pl
from jax.experimental.pallas import tpu as pltpu
from jax.sharding import PartitionSpec as P

MESH = pl.DeviceIdType.MESH
f32 = jnp.float32
bf = jnp.bfloat16
VMEM_LIMIT = 67043328


def mm(a, b):
    return lax.dot_general(a, b, (((1,), (0,)), ((), ())), preferred_element_type=f32)


def mmt(a, b):
    return lax.dot_general(a, b, (((1,), (1,)), ((), ())), preferred_element_type=f32)


def kernel(
    x_in, dy_in, wg_in, wu_in, wd_in,
    y_out, dx_out, dw_out, zl, far_r, near, xr1, yr1, xr2, yr2,
    wg, wu, wd, xa, dya, act, zs, zin, lt, fst, nst, cst, ost,
    gs, gr, lsem, zsend, zrecv, zload, fsend, frecv, nstore, cload, xs1, xq1, ys1, yq1, xs2, xq2, ys2, yq2, cin, osem,
):
    tp = lax.axis_index("tp")
    dp = lax.axis_index("dp")
    z, y = tp // 2, tp % 2
    x, c = dp // 2, dp % 2
    nxt = 2 * z + 1 - 5 * (z // 2)
    prv = z // 2 + 2 * (1 - z % 2)
    dev_x = {"tp": tp, "dp": 2 * (1 - x) + c}
    dev_y = {"tp": 2 * z + 1 - y, "dp": dp}
    dev_c = {"tp": tp, "dp": 2 * x + 1 - c}
    dev_n = {"tp": 2 * nxt + y, "dp": dp}
    dev_p = {"tp": 2 * prv + y, "dp": dp}

    nr, d = x_in.shape
    kd, kf = wg_in.shape
    f = 2 * kf
    hd = kd // 2

    def nat(r):
        rc, rx = r // 2, r % 2
        return 2 * (x + rx - 2 * x * rx) + c + rc - 2 * c * rc

    def ncol(r):
        return pl.ds(pl.multiple_of(nat(r) * kd, kd), kd)

    def remote(src, dst, ss, rs, dev):
        return pltpu.make_async_remote_copy(
            src_ref=src, dst_ref=dst, send_sem=ss, recv_sem=rs, device_id=dev, device_id_type=MESH
        )

    local = []
    for r in range(4):
        local.append((x_in.at[:, ncol(r)], xa.at[0, :, pl.ds(r * kd, kd)]))
        local.append((dy_in.at[:, ncol(r)], dya.at[0, :, pl.ds(r * kd, kd)]))
    own = (wg_in, wu_in, wd_in)

    def blk(k, rx, rc, ry, h=None):
        d0 = (2 * rc + rx) * kd
        if k < 2:
            ref = (wg, wu)[k]
            if h is None:
                return ref.at[pl.ds(d0, kd), pl.ds(ry * kf, kf)]
            return ref.at[pl.ds(d0 + h * hd, hd), pl.ds(ry * kf, kf)]
        if h is None:
            return wd.at[pl.ds(ry * kf, kf), pl.ds(d0, kd)]
        return wd.at[pl.ds(ry * kf + h * (kf // 2), kf // 2), pl.ds(d0, kd)]

    for k in range(3):
        local.append((own[k], blk(k, 0, 0, 0)))
    local = [pltpu.make_async_copy(s, t, lsem.at[i]) for i, (s, t) in enumerate(local)]
    for cp in local:
        cp.start()

    bar = pltpu.get_barrier_semaphore()
    for dev in (dev_x, dev_y, dev_c, dev_n, dev_p):
        pl.semaphore_signal(bar, inc=1, device_id=dev, device_id_type=MESH)
    pl.semaphore_wait(bar, 5)

    count = [0]
    sends = []

    def send(src, dst, dev):
        i = count[0]
        count[0] += 1
        cp = remote(src, dst, gs.at[i], gr.at[i], dev)
        cp.start()
        sends.append(cp)
        return cp

    zc = [[None, None] for _ in range(3)]
    xc, yc, cc = [None] * 3, [None] * 3, []
    for k in range(3):
        xc[k] = send(own[k], blk(k, 1, 0, 0), dev_x)
        yc[k] = send(own[k], blk(k, 0, 0, 1), dev_y)
        cc.append(send(own[k], blk(k, 0, 1, 0), dev_c))
    for cp in local[:8]:
        cp.wait()
    zc[0][0] = send(xa.at[0], xa.at[1], dev_n)
    zc[0][1] = send(dya.at[0], dya.at[1], dev_n)

    def zstep(s, j):
        ref = (xa, dya)[j]
        zc[s - 1][j].wait_recv()
        if s < 3:
            zc[s][j] = send(ref.at[s], ref.at[s + 1], dev_n)

    ra, rb = [None] * 3, [None] * 3
    for k in range(3):
        xc[k].wait_recv()
        ra[k] = send(blk(k, 1, 0, 0, 0), blk(k, 1, 0, 1, 0), dev_y)
        yc[k].wait_recv()
        rb[k] = send(blk(k, 0, 0, 1, 1), blk(k, 1, 0, 1, 1), dev_x)
        cc.append(send(blk(k, 1, 0, 0), blk(k, 1, 1, 0), dev_c))
        cc.append(send(blk(k, 0, 0, 1), blk(k, 0, 1, 1), dev_c))
        zstep(*((1, 0), (1, 1), (2, 0))[k])
    for k in range(3):
        if k == 2:
            zstep(2, 1)
        ra[k].wait_recv()
        cc.append(send(blk(k, 1, 0, 1, 0), blk(k, 1, 1, 1, 0), dev_c))
        rb[k].wait_recv()
        cc.append(send(blk(k, 1, 0, 1, 1), blk(k, 1, 1, 1, 1), dev_c))
    for cp in local[8:]:
        cp.wait()
    for cp in cc:
        cp.wait_recv()

    ft = min(256, f)

    def rows(s):
        return pl.ds(s * nr, nr)

    def front(s):
        @pl.loop(0, f // ft)
        def _(i):
            col = pl.ds(pl.multiple_of(i * ft, ft), ft)
            a = mm(xa[s], wg[:, col])
            b = mm(xa[s], wu[:, col])
            g = mmt(dya[s], wd[col, :])
            sig = jax.nn.sigmoid(a)
            sa = a * sig
            act[2, rows(s), col] = (sa * b).astype(bf)
            act[0, rows(s), col] = (g * b * sig * (1.0 + a * (1.0 - sig))).astype(bf)
            act[1, rows(s), col] = (g * sa).astype(bf)

    def back_y(s, r):
        return mm(act[2, rows(s), :], wd[:, pl.ds(pl.multiple_of(r * kd, kd), kd)])

    def back_dx(s, r):
        row = pl.ds(pl.multiple_of(r * kd, kd), kd)
        return mmt(act[0, rows(s), :], wg[row, :]) + mmt(act[1, rows(s), :], wu[row, :])

    def zcopy(step, i):
        return remote(zs.at[i], zl.at[step, i], zsend.at[i], zrecv.at[step, i], dev_n)

    def zinload(step, i):
        return pltpu.make_async_copy(zl.at[step, i], zin.at[i % 2], zload.at[i % 2])

    def zpart(s, kind):
        calc = (back_y, back_dx)[kind]

        @pl.loop(0, 4)
        def _(r):
            i = 4 * kind + r
            if s > 1:
                zcopy(s - 2, i).wait_recv()
                zinload(s - 2, i).start()
            v = calc(s, r)
            if s > 1:
                zinload(s - 2, i).wait()
                v = v + zin[i % 2]
                zcopy(s - 2, i).wait_send()
            zs[i] = v

            @pl.when(r > 0)
            def _():
                zcopy(s - 1, i - 1).start()

    def zlast(s, kind):
        zcopy(s - 1, 4 * kind + 3).start()

    def zend(kind):
        calc = (back_y, back_dx)[kind]
        src, out = ((xa, y_out), (dya, dx_out))[kind]

        def store(r):
            return pltpu.make_async_copy(ost.at[r % 2], out.at[:, ncol(r)], osem.at[r % 2])

        @pl.loop(0, 4)
        def _(r):
            i = 4 * kind + r
            v = calc(0, r)
            zcopy(2, i).wait_recv()
            zinload(2, i).start()
            v = v + src[0, :, pl.ds(pl.multiple_of(r * kd, kd), kd)].astype(f32)
            zinload(2, i).wait()

            @pl.when(r > 1)
            def _():
                store(r).wait()

            ost[r % 2] = (v + zin[i % 2]).astype(bf)
            store(r).start()

        store(2).wait()
        store(3).wait()

    def transpose(rc, rx):
        c0 = (2 * rc + rx) * kd
        for l, ref in ((0, xa), (1, dya)):
            for s in range(4):
                lt[l, :, rows(s)] = ref[s, :, pl.ds(c0, kd)].T

    def unit(j):
        ryi, k, half = j // 6, (j // 2) % 3, j % 2
        a = lt[k // 2, pl.ds(pl.multiple_of(half * hd, hd), hd), :]
        b = act[k, :, pl.ds(pl.multiple_of((1 - ryi) * kf, kf), kf)]
        return mm(a, b)

    def fcopy(u):
        return remote(fst.at[u % 2], far_r.at[u], fsend.at[u % 2], frecv.at[u], dev_c)

    def far(rx):
        base = 12 * (1 - rx)
        transpose(1, rx)

        @pl.loop(0, 12)
        def _(j):
            u = base + j
            v = unit(j)

            @pl.when(u > 1)
            def _():
                fcopy(u).wait_send()

            fst[u % 2] = v

            @pl.when(j > 0)
            def _():
                fcopy(u - 1).start()

        fcopy(base + 11).start()

    def ncopy(u):
        return pltpu.make_async_copy(nst.at[u % 2], near.at[u], nstore.at[u % 2])

    def xcopy1(i, u):
        return remote(near.at[u], xr1.at[i], xs1.at[i], xq1.at[i], dev_x)

    def ycopy1(i, u):
        return remote(near.at[u], yr1.at[i], ys1.at[i], yq1.at[i], dev_y)

    def nsend(rx, j):
        ryi, k, half = j // 6, (j // 2) % 3, j % 2
        u = 12 * (1 - rx) + j
        if rx:
            @pl.when(half == 0)
            def _():
                xcopy1(ryi * 3 + k, u).start()

        @pl.when((half == 1) & (ryi == 0))
        def _():
            ycopy1(3 * (1 - rx) + k, u).start()

    def nearg(rx):
        base = 12 * (1 - rx)
        transpose(0, rx)

        @pl.loop(0, 12)
        def _(j):
            u = base + j
            fcopy(u).wait_recv()
            cp = pltpu.make_async_copy(far_r.at[u], cst, cload)
            cp.start()
            v = unit(j)
            cp.wait()
            nst[u % 2] = v + cst[...]

            @pl.when(j > 0)
            def _():
                ncopy(u - 1).wait()
                nsend(rx, j - 1)

            ncopy(u).start()

        ncopy(base + 11).wait()
        nsend(rx, 11)

    def gather_sum(srcs, dst):
        bufs = (fst.at[0], fst.at[1], cst)
        cps = [pltpu.make_async_copy(s, b, cin.at[i]) for i, (s, b) in enumerate(zip(srcs, bufs))]
        for cp in cps:
            cp.start()
        for cp in cps:
            cp.wait()

        st = min(64, hd)

        @pl.loop(0, hd // st)
        def _(i):
            row = pl.ds(pl.multiple_of(i * st, st), st)
            v = fst[0, row, :] + fst[1, row, :]
            if len(srcs) == 3:
                v = v + cst[row, :]
            nst[0, row, :] = v

        cp = pltpu.make_async_copy(nst.at[0], dst, nstore.at[0])
        cp.start()
        cp.wait()

    def uid(rx, ry, k, half):
        return 12 * (1 - rx) + 6 * (1 - ry) + 2 * k + half

    def second(k):
        ua, ub = uid(0, 1, k, 0), uid(1, 0, k, 1)
        xcopy1(k, 0).wait_recv()
        gather_sum((near.at[ua], xr1.at[k]), near.at[ua])
        ca = remote(near.at[ua], yr2.at[k], ys2.at[k], yq2.at[k], dev_y)
        ca.start()
        ycopy1(k, 0).wait_recv()
        gather_sum((near.at[ub], yr1.at[k]), near.at[ub])
        cb = remote(near.at[ub], xr2.at[k], xs2.at[k], xq2.at[k], dev_x)
        cb.start()
        return ca, cb

    def last(k, ca, cb):
        xcopy1(3 + k, 0).wait_recv()
        ca.wait_recv()
        gather_sum((near.at[uid(0, 0, k, 0)], xr1.at[3 + k], yr2.at[k]), dw_out.at[k, pl.ds(0, hd)])
        ycopy1(3 + k, 0).wait_recv()
        cb.wait_recv()
        gather_sum((near.at[uid(0, 0, k, 1)], yr1.at[3 + k], xr2.at[k]), dw_out.at[k, pl.ds(hd, hd)])

    front(1)
    zpart(1, 0)
    zlast(1, 0)
    zpart(1, 1)
    zlast(1, 1)
    front(0)
    front(2)
    zstep(3, 0)
    zstep(3, 1)
    front(3)
    far(1)
    nearg(1)
    far(0)
    nearg(0)
    fcopy(0).wait_send()
    fcopy(1).wait_send()
    zpart(2, 0)
    zlast(2, 0)
    zpart(2, 1)
    zlast(2, 1)
    pairs = [second(k) for k in range(3)]
    zpart(3, 0)
    zlast(3, 0)
    zpart(3, 1)
    zlast(3, 1)
    zend(0)
    for k in range(3):
        last(k, *pairs[k])
    zend(1)

    for cp in sends:
        cp.wait_send()
    for i in range(8):
        zcopy(2, i).wait_send()
    for i in range(6):
        xcopy1(i, 0).wait_send()
        ycopy1(i, 0).wait_send()
    for ca, cb in pairs:
        ca.wait_send()
        cb.wait_send()


def fused(x, dy, wg, wu, wd):
    nr, d = x.shape
    kd, kf = wg.shape
    f, hd = 2 * kf, kd // 2
    hbm = pl.BlockSpec(memory_space=pl.ANY)
    sds = jax.ShapeDtypeStruct
    ng = 33
    out_shape = (
        sds((nr, d), bf), sds((nr, d), bf), sds((3, kd, kf), f32),
        sds((3, 8, nr, kd), f32), sds((24, hd, kf), f32), sds((24, hd, kf), f32),
        sds((6, hd, kf), f32), sds((6, hd, kf), f32), sds((3, hd, kf), f32), sds((3, hd, kf), f32),
    )
    dma = pltpu.SemaphoreType.DMA
    return pl.pallas_call(
        kernel,
        name="fused",
        out_shape=out_shape,
        in_specs=[hbm] * 5,
        out_specs=(hbm,) * len(out_shape),
        scratch_shapes=[
            pltpu.VMEM((d, f), bf), pltpu.VMEM((d, f), bf), pltpu.VMEM((f, d), bf),
            pltpu.VMEM((4, nr, d), bf), pltpu.VMEM((4, nr, d), bf), pltpu.VMEM((3, 4 * nr, f), bf),
            pltpu.VMEM((8, nr, kd), f32), pltpu.VMEM((2, nr, kd), f32), pltpu.VMEM((2, kd, 4 * nr), bf),
            pltpu.VMEM((2, hd, kf), f32), pltpu.VMEM((2, hd, kf), f32), pltpu.VMEM((hd, kf), f32),
            pltpu.VMEM((2, nr, kd), bf),
            dma((ng,)), dma((ng,)), dma((11,)), dma((8,)), dma((3, 8)), dma((2,)), dma((2,)), dma((24,)), dma((2,)), dma,
            dma((6,)), dma((6,)), dma((6,)), dma((6,)), dma((3,)), dma((3,)), dma((3,)), dma((3,)), dma((3,)), dma((2,)),
        ],
        compiler_params=pltpu.CompilerParams(collective_id=0, has_side_effects=True, vmem_limit_bytes=VMEM_LIMIT),
    )(x, dy, wg, wu, wd)


def solution(mesh):
    rows = P(("dp", "tp"), None)
    wsp = P("dp", "tp")
    dsp = P("tp", "dp")

    def local(x, w_gate, w_up, w_down, dy):
        y, dx, dw = fused(x, dy, w_gate, w_up, w_down)[:3]
        return y, dx, dw[0], dw[1], dw[2].T

    return jax.shard_map(local, mesh=mesh, in_specs=(rows, wsp, wsp, dsp, rows), out_specs=(rows, rows, wsp, wsp, dsp), check_vma=False)
```

time: 1910 us -> 464 us (0.24)
  waiting for transfers between devices: 1610 us -> 0 us
  Pallas kernels: 0 us -> 451 us
  matrix products: 132 us -> 0 us
  local copies, waits for them, and re-layouts: 70.4 us -> 10.9 us
  blocking collectives: 36.2 us -> 0 us
  other arithmetic: 28.3 us -> 0 us
    reduce_scatter x4 -> x0, waiting for transfers between devices: 1140 us -> none  [the longest x2 497 us: combine_tp(): lax.psum_scatter(q.reshape(nx, ny, tl, dl), 'tp', scatter_dimension=1, ti...]
    all_gather x4 -> x0, waiting for transfers between devices: 468 us -> none  [the longest x2 199 us: all_tokens(): vg = lax.all_gather(va, 'tp', axis=0, tiled=False)]
    pallas_call x0 -> x1, Pallas kernels: none -> 451 us  [fused(): pl.pallas_call(kernel, name='fused', out_shape=out_shape, in_specs=[hbm]...]
    dot_general x6 -> x0, matrix products: 132 us -> none  [the longest x1 31.1 us: local(): jnp.dot(xt, w, preferred_element_type=f32)]
    all_to_all x2 -> x0, blocking collectives: 36.2 us -> none  [to_columns(): return lax.all_to_all(vr, 'dp', 0, 0, tiled=True)]
    reshape x2 -> x0, local copies, waits for them, and re-layouts: 34.7 us -> none  [combine_tp(): q.reshape(nx, ny, tl, dl)]
    convert_element_type x3 -> x0, other arithmetic: 20 us -> none  [the longest x1 14.3 us: local(): da = (g * b * sig * (1.0 + a * (1.0 - sig))).astype(bf)]
  transfers between devices with their start and end apart: 10 -> 0, of which waited for: 8 -> 0; matrix products, arithmetic and copies ran while one was open for 11% -> 0% of each run, Pallas kernels for 0% -> 0%
where the time goes in v1:
time: 464 us; the launch traced here: 462 us
  Pallas kernels  451 us (97%)
  local copies, waits for them, and re-layouts  10.9 us (2%)
    pallas_call x1, Pallas kernels, fused(): pl.pallas_call(kernel, name='fused', out_shape=out_shape, in_specs=[hbm]...  451 us

profile of v1, /device:TPU:0, one launch (start us, length us, event | category | flops | bytes accessed | tf_op | source)
XLA Modules:
  0.0 462.2 jit_solution(12885602603553496819)
XLA Ops:
  0.6 450.6 %fused.1 = (bf16[256,2048]{1,0:T(8,128)(2,1)}, bf16[256,2048]{1,0:T(8,128)(2,1)}, f32[3,512,1024]{2,1,0:T(8,128)}, f32[3,8,256,512]{3,2,1,0:T(8,128)}, f32[24,25...) custom-call(bf16[256,2048]{1,0:T(8,128)(2,1)} %x_in.1, ...), custom_call_target="tpu_custom_call" | custom-call | tf_op jit(solution)/shard_map/fused/pallas_call | solution.py:395
  451.3 5.8 %slice_bitcast_fusion = (f32[1024,512]{0,1:T(8,128)S(1)}, f32[512,1024]{1,0:T(8,128)}, f32[512,1024]{1,0:T(8,128)}) fusion(f32[3,512,1024]{2,1,0:T(8,128)} %get-tuple-element.10), kind=kLoop, calls=%fused_computation | loop fusion | bytes 12582912 | tf_op jit(solution)/shard_map/transpose | solution.py:421
  457.1 0.0 copy-start
  457.1 1.8 copy.10
  458.9 2.3 copy.13
  461.2 0.0 copy-done
  461.2 1.0 copy.14
Async XLA Ops:
  457.1 4.1 copy-start
